TPU v7x, 32 devices: a whole 2x2x4 slice. The times are simulated.
32 devices in a mesh: out: 8 (over z, x), inp: 4 (over y, core).
Axes of the slice: x: 2, y: 2, z: 4, core: 2. Of those that a mesh axis runs over, the one named last changes fastest.
Arguments:
- tensor: bfloat16 [1024, 1024, 1024], P('out', 'inp'), may hold values from -0.005859375 to 0.005859375
- state: bfloat16 [768, 1024], P('out'), may hold values from -6 to 6
Outputs:
- collision: bfloat16 [768, 1024], P('inp', 'out')
All inputs are finite; a program needn't handle non-finite values.
Results may differ from a plain program's by a relative error of at most 0.001.
Values may be sent and summed in bfloat16 or wider, within the bound.
A program may use at most 128 MiB of HBM per device.

v0:
```python
import jax
import jax.numpy as jnp
from jax import lax
from jax.sharding import PartitionSpec as P


def local(tensor, state):
    rows_out = tensor.shape[0]
    rows_inp = tensor.shape[1]
    width = tensor.shape[2]
    flat = tensor.reshape(rows_out * rows_inp, width)
    first_col = lax.axis_index("inp") * rows_inp
    piece = lax.all_gather(state, "out", axis=0, tiled=True)
    inner = lax.dot_general(
        piece, flat, (((1,), (1,)), ((), ())), preferred_element_type=jnp.float32
    )
    inner = inner.reshape(piece.shape[0], rows_out, rows_inp)
    chosen = lax.dynamic_slice_in_dim(piece, first_col, rows_inp, 1).astype(jnp.float32)
    partial_sum = jnp.sum(inner * chosen[:, None, :], axis=2)
    owned = lax.psum_scatter(partial_sum, "inp", scatter_dimension=0, tiled=True)
    return owned.astype(jnp.bfloat16)


def solution(mesh):
    placed = (P("out", "inp", None), P("out", None))
    return jax.shard_map(
        local, mesh=mesh, in_specs=placed, out_specs=P("inp", "out"), check_vma=False
    )
```

profile of v0, /device:TPU:0, one launch (start us, length us, event | category | flops | bytes accessed | tf_op | source)
XLA Modules:
  0.0 146.9 jit_solution(9233174708893492193)
XLA Ops:
  6.5 0.0 all-gather.2.cloned.1.call-start
  6.5 0.7 all-gather.2.cloned.1.call-update
  7.3 0.0 reduce-scatter.4.cloned.1.call-start
  7.3 49.1 %all-gather.2.cloned.1.call-done = bf16[768,1024]{1,0:T(8,128)(2,1)} async-done(((bf16[96,1024]{1,0:T(8,128)(2,1)}), bf16[768,1024]{1,0:T(8,128)(2,1)}) %all-gather.2.cloned.1.call-update) | async-done | bytes 1572880 | tf_op jit(solution)/shard_map/all_gather | solution.py:13
  56.4 1.0 dynamic-slice_convert_fusion
  57.5 0.3 copy.8
  57.8 60.4 %multiply_reduce_fusion = f32[768,128]{0,1:T(8,128)S(1)} fusion(f32[768,256]{0,1:T(8,128)S(1)} %copy.8, bf16[128,256,1024]{2,1,0:T(8,128)(2,1)} %param.2, bf16[768,1024]{1,0:T(8,128)(2,1)} %all-gather.2.cloned.1.call-done), kind=kOutput, calls=%fused_computation | convolution fusion | flops 51589840896 | bytes 69861376 | tf_op jit(solution)/shard_map/dot_general | solution.py:14
  118.2 0.9 copy.10
  119.1 0.0 reduce-scatter.4.cloned.1.call-update
  119.1 19.3 %reduce-scatter.4.cloned.1.call-done = f32[192,128]{1,0:T(8,128)} async-done(((f32[768,128]{1,0:T(8,128)}), f32[192,128]{1,0:T(8,128)}) %reduce-scatter.4.cloned.1.call-update) | async-done | bytes 98320 | tf_op jit(solution)/shard_map/reduce_scatter | solution.py:20
  138.5 1.5 %convert_element_type.7 = bf16[192,128]{1,0:T(8,128)(2,1)} convert(f32[192,128]{1,0:T(8,128)} %reduce-scatter.4.cloned.1.call-done) | non-fusion elementwise | flops 24576 | bytes 147456 | tf_op jit(solution)/shard_map/convert_element_type | solution.py:21
Async XLA Ops:
  6.5 49.9 %all-gather.2.cloned.1.call-start = ((), (), s32[]{:S(2)}) async-start(), calls=%async_computation.1 | async-start | bytes 1769472 | tf_op jit(solution)/shard_map/all_gather | solution.py:13
  7.3 131.2 %reduce-scatter.4.cloned.1.call-start = ((), (), s32[]{:S(2)}) async-start(), calls=%async_computation.2 | async-start | bytes 491520 | tf_op jit(solution)/shard_map/reduce_scatter | solution.py:20
Sparse Core Ops, SparseCore 0:
  9.5 46.8 all-gather.1
  119.3 19.1 reduce-scatter.3
where the time goes:
time: 147 us
  waiting for transfers between devices  69.2 us (47%)
  matrix products  60.4 us (41%)
  between operations  13.4 us (9%)
  other arithmetic  2.56 us (2%)
    dot_general x1, matrix products, local(): lax.dot_general(piece, flat, (((1,), (1,)), ((), ())), preferred_element_...  60.4 us
    all_gather x1, waiting for transfers between devices, local(): piece = lax.all_gather(state, 'out', axis=0, tiled=True)  49.1 us
    reduce_scatter x1, waiting for transfers between devices, local(): lax.psum_scatter(partial_sum, 'inp', scatter_dimension=0, tiled=True)  19.3 us
  transfers between devices with their start and end apart: 2, of which 2 were waited for; matrix products, arithmetic and copies ran while one was open for 0% of the time, Pallas kernels for 0%

commit v1 on v0

--- a/solution.py
+++ b/solution.py
@@ -10,7 +10,12 @@
     width = tensor.shape[2]
     flat = tensor.reshape(rows_out * rows_inp, width)
     first_col = lax.axis_index("inp") * rows_inp
-    piece = lax.all_gather(state, "out", axis=0, tiled=True)
+    sheets = []
+    for _ in range(lax.axis_size("out")):
+        sheets.append(state)
+    carry_out = jnp.stack(sheets, axis=0)
+    even = lax.all_to_all(carry_out, "out", 0, 0)
+    piece = jnp.concatenate(even, axis=0)
     inner = lax.dot_general(
         piece, flat, (((1,), (1,)), ((), ())), preferred_element_type=jnp.float32
     )

time: 147 us -> 143 us (0.973)
  waiting for transfers between devices: 69.2 us -> 57 us
  starting transfers between devices: 0.04 us -> 7.32 us
  local copies, waits for them, and re-layouts: 1.17 us -> 3.44 us
    all_gather x1 -> x0, waiting for transfers between devices: 49.1 us -> none  [local(): piece = lax.all_gather(state, 'out', axis=0, tiled=True)]
    all_to_all x0 -> x1, waiting for transfers between devices: none -> 37 us  [local(): even = lax.all_to_all(carry_out, 'out', 0, 0)]
    all_to_all x0 -> x1, starting transfers between devices: none -> 7.28 us  [local(): even = lax.all_to_all(carry_out, 'out', 0, 0)]
    another operation x0 -> x1, local copies, waits for them, and re-layouts: none -> 2.27 us  [local(): carry_out = jnp.stack(sheets, axis=0)]
where the time goes in v1:
time: 143 us
  matrix products  60 us (42%)
  waiting for transfers between devices  57 us (40%)
  between operations  13.4 us (9%)
  starting transfers between devices  7.32 us (5%)
  local copies, waits for them, and re-layouts  3.44 us (2%)
  other arithmetic  1.58 us (1%)
    dot_general x1, matrix products, local(): lax.dot_general(piece, flat, (((1,), (1,)), ((), ())), preferred_element_...  60 us
    all_to_all x1, waiting for transfers between devices, local(): even = lax.all_to_all(carry_out, 'out', 0, 0)  37 us
    reduce_scatter x1, waiting for transfers between devices, local(): lax.psum_scatter(partial_sum, 'inp', scatter_dimension=0, tiled=True)  20 us
    all_to_all x1, starting transfers between devices, local(): even = lax.all_to_all(carry_out, 'out', 0, 0)  7.28 us
  transfers between devices with their start and end apart: 2, of which 2 were waited for; matrix products, arithmetic and copies ran while one was open for 0% of the time, Pallas kernels for 0%

profile of v1, /device:TPU:0, one launch (start us, length us, event | category | flops | bytes accessed | tf_op | source)
XLA Modules:
  0.0 142.8 jit_solution(1464231651176460217)
XLA Ops:
  6.5 2.3 %stack.2 = bf16[8,96,1024]{2,1,0:T(8,128)(2,1)} broadcast(bf16[96,1024]{1,0:T(8,128)(2,1)} %param.3), dimensions={1,2} | broadcast | bytes 1769472 | tf_op jit(solution)/shard_map/stack | solution.py:16
  8.8 7.3 %all-to-all-start = ((bf16[8,96,1024]{2,1,0:T(8,128)(2,1)}), bf16[8,96,1024]{2,1,0:T(8,128)(2,1)S(1)}, u32[]{:S(2)}, u32[]{:S(2)}) async-start(bf16[8,96,1024]{2,1,0:T(8,128)(2,1)} %stack.2), calls=%async_computation | async-start | bytes 3145728 | tf_op jit(solution)/shard_map/all_to_all | solution.py:17
  16.1 0.0 reduce-scatter.4.cloned.1.call-start
  16.1 37.0 %all-to-all-done = bf16[8,96,1024]{2,1,0:T(8,128)(2,1)S(1)} async-done(((bf16[8,96,1024]{2,1,0:T(8,128)(2,1)}), bf16[8,96,1024]{2,1,0:T(8,128)(2,1)S(1)}, u32[]{:S(2)}, u32[]{:S(2)}) %all-to-all-start) | async-done | bytes 1572896 | tf_op jit(solution)/shard_map/all_to_all | solution.py:17
  53.1 0.1 dynamic-slice_convert_fusion
  53.2 0.3 copy.8
  53.4 60.0 %multiply_reduce_fusion = f32[768,128]{0,1:T(8,128)S(1)} fusion(f32[768,256]{0,1:T(8,128)S(1)} %copy.8, bf16[768,1024,1]{1,0,2:T(8,128)(2,1)S(1)} %bitcast.7, bf16[128,256,1024]{2,1,0:T(8,128)(2,1)} %param.2), kind=kOutput, calls=%fused_computation | convolution fusion | flops 51589840896 | bytes 69861376 | tf_op jit(solution)/shard_map/dot_general | solution.py:19
  113.4 0.9 copy.10
  114.3 0.0 reduce-scatter.4.cloned.1.call-update
  114.4 20.0 %reduce-scatter.4.cloned.1.call-done = f32[192,128]{1,0:T(8,128)} async-done(((f32[768,128]{1,0:T(8,128)}), f32[192,128]{1,0:T(8,128)}) %reduce-scatter.4.cloned.1.call-update) | async-done | bytes 98320 | tf_op jit(solution)/shard_map/reduce_scatter | solution.py:25
  134.4 1.5 %convert_element_type.7 = bf16[192,128]{1,0:T(8,128)(2,1)} convert(f32[192,128]{1,0:T(8,128)} %reduce-scatter.4.cloned.1.call-done) | non-fusion elementwise | flops 24576 | bytes 147456 | tf_op jit(solution)/shard_map/convert_element_type | solution.py:26
Async XLA Ops:
  8.8 44.3 %all-to-all-start = ((bf16[8,96,1024]{2,1,0:T(8,128)(2,1)}), bf16[8,96,1024]{2,1,0:T(8,128)(2,1)S(1)}, u32[]{:S(2)}, u32[]{:S(2)}) async-start(bf16[8,96,1024]{2,1,0:T(8,128)(2,1)} %stack.2), calls=%async_computation | async-start | bytes 3145728 | tf_op jit(solution)/shard_map/all_to_all | solution.py:17
  16.1 118.3 %reduce-scatter.4.cloned.1.call-start = ((), (), s32[]{:S(2)}) async-start(), calls=%async_computation.2 | async-start | bytes 491520 | tf_op jit(solution)/shard_map/reduce_scatter | solution.py:25
Sparse Core Ops, SparseCore 0:
  114.5 19.8 reduce-scatter.3
